TPU v7x, 32 devices: a whole 2x2x4 slice. The times are simulated.
32 devices in a mesh: band: 8 (over y, x, core), pw: 4 (over z).
Axes of the slice: x: 2, y: 2, z: 4, core: 2. Of those that a mesh axis runs over, the one named last changes fastest.
Arguments:
- pair_density: bfloat16 [40, 128, 9216], P('band', None, 'pw'), may hold values from -6 to 6
- eigvecs: bfloat16 [2944, 9216], P('band', 'pw'), may hold values from -0.0625 to 0.0625
- screening: bfloat16 [2944, 2944], P('pw'), may hold values from -0.00048828125 to 0.00048828125
- occupation: float32 [16], replicated, may hold values from 0 to 1
- window_start: int32 [40], P('band'), may hold values from 0 to 511, as said below
- window_len: int32 [40], P('band'), may hold values from 1 to 128, as said below
- slot_band: int32 [40], P('band'), may hold values from -1 to 15, as said below
Outputs:
- sigma: float32 [512, 512], P(('band', 'pw'))
Inputs may be any that keep to these rules, and one draw needn't show every extreme that they name: window_start + window_len <= 512 for every slot. `window_len`: some slot has a window of 128 bands. On each index of band the live slots (slot_band >= 0) come first among its 5 slots; each index holds 3 to 5 live slots, and the counts of index i and index i + 8 / 2 add up to 8.
All inputs are finite; a program needn't handle non-finite values.
Results may differ from a plain program's by a relative error of at most 0.0049.
Values may be sent and summed in bfloat16 or wider, within the bound.
A program may use at most 128 MiB of HBM per device.

v0:
```python
import jax
import jax.numpy as jnp
from jax import lax
from jax.sharding import PartitionSpec as P

NB_SIGMA = 512


def per_device(pair_density, eigvecs, screening, occupation, window_start, window_len, slot_band):
    capacity, block, plane_rows = pair_density.shape
    density, starts, lengths, band_ids = (pair_density, window_start, window_len, slot_band)
    slots = density.shape[0]
    flat = density.reshape(slots * block, plane_rows)
    partial_proj = lax.dot_general(
        flat,
        lax.all_gather(eigvecs, "band", axis=0, tiled=True),
        (((1,), (1,)), ((), ())),
        preferred_element_type=jnp.float32,
    )
    row_ids = jnp.arange(block, dtype=jnp.int32)
    keep_rows = ((row_ids[None, :] < lengths[:, None]) & (band_ids[:, None] >= 0)).astype(
        jnp.float32
    )
    masked = partial_proj * keep_rows.reshape(slots * block, 1)
    projected = lax.psum(masked, "pw").astype(jnp.bfloat16)
    width = screening.shape[0]
    own_cols = lax.dynamic_slice_in_dim(projected, lax.axis_index("pw") * width, width, 1)
    screened = lax.dot_general(
        projected, screening, (((1,), (1,)), ((), ())), preferred_element_type=jnp.float32
    ).astype(jnp.bfloat16)
    block_sigma = lax.dot_general(
        screened.reshape(slots, block, width),
        own_cols.reshape(slots, block, width),
        (((2,), (2,)), ((0,), (0,))),
        preferred_element_type=jnp.float32,
    )
    band_list = jnp.arange(occupation.shape[0], dtype=jnp.int32)
    weights = 0.5 - jnp.sum(
        jnp.where(band_list[None, :] == band_ids[:, None], occupation[None, :], 0.0), axis=1
    )
    totals = jnp.zeros((NB_SIGMA + block, NB_SIGMA + block), jnp.float32)
    for index in range(slots):
        first = starts[index]
        previous = lax.dynamic_slice(totals, (first, first), (block, block))
        totals = lax.dynamic_update_slice(
            totals, previous + weights[index] * block_sigma[index], (first, first)
        )
    sigma_part = totals[:NB_SIGMA, :NB_SIGMA]
    by_band = lax.psum_scatter(sigma_part, "band", scatter_dimension=0, tiled=True)
    return lax.psum_scatter(by_band, "pw", scatter_dimension=0, tiled=True)


def solution(mesh):
    return jax.shard_map(
        per_device,
        mesh=mesh,
        in_specs=(
            P("band", None, "pw"),
            P("band", "pw"),
            P("pw", None),
            P(),
            P("band"),
            P("band"),
            P("band"),
        ),
        out_specs=P(("band", "pw"), None),
        check_vma=False,
    )
```

profile of v0, /device:TPU:0, one launch (start us, length us, event | category | flops | bytes accessed | tf_op | source)
XLA Modules:
  0.0 465.4 jit_solution(47097493405840025)
XLA Ops:
  6.5 0.0 copy-start
  6.5 0.0 all-gather.2.cloned.1.call-start
  6.5 0.7 all-gather.2.cloned.1.call-update
  7.3 0.0 reduce-scatter.3.cloned.1.call-start
  7.3 1.4 fusion.11
  17.9 0.9 select_reduce_fusion
  18.7 0.7 fusion.10
  19.4 0.7 broadcast_compare_fusion
  20.1 0.7 convert_bitcast_fusion
  20.8 67.3 %all-gather.2.cloned.1.call-done = bf16[2944,2304]{1,0:T(8,128)(2,1)} async-done(((bf16[368,2304]{1,0:T(8,128)(2,1)}), bf16[2944,2304]{1,0:T(8,128)(2,1)}) %all-gather.2.cloned.1.call-update) | async-done | bytes 13565968 | tf_op jit(solution)/shard_map/all_gather | solution.py:16
  88.1 0.0 copy-done
  88.1 14.4 %convolution_multiply_fusion = f32[640,2944]{1,0:T(8,128)} fusion(bf16[640,2304]{1,0:T(8,128)(2,1)S(1)} %bitcast.39, bf16[2944,2304]{1,0:T(8,128)(2,1)} %all-gather.2.cloned.1.call-done, f32[640]{0:T(1024)S(1)} %convert_bitcast_fusion), kind=kOutput, calls=%fused_computation | convolution fusion | flops 8684093440 | bytes 24054272 | tf_op jit(solution)/shard_map/dot_general | solution.py:14
  102.5 259.2 %all-reduce.1 = bf16[640,2944]{1,0:T(8,128)(2,1)} all-reduce(f32[640,2944]{1,0:T(8,128)} %convolution_multiply_fusion), channel_id=1, replica_groups=mesh['band'=8,'pw'=4] {'pw'}, use_global_device_ids=true, to_apply=%region_1.2 | all-reduce | flops 1884160 | bytes 11304960 | tf_op jit(solution)/shard_map/psum | solution.py:25
  361.7 2.7 constant_dynamic-slice_fusion
  364.4 8.0 %convolution_convert_fusion = bf16[640,736]{0,1:T(8,128)(2,1)} fusion(bf16[640,2944]{1,0:T(8,128)(2,1)} %all-reduce.1, bf16[736,2944]{1,0:T(8,128)(2,1)} %param.9), kind=kOutput, calls=%fused_computation.1 | convolution fusion | flops 2773954560 | bytes 9043968 | tf_op jit(solution)/shard_map/dot_general | solution.py:28
  372.4 2.2 copy.12
  374.7 1.9 fusion.12
  376.6 0.7 fusion.8
  377.3 1.3 broadcast_in_dim.10
  378.6 3.0 dynamic_update_slice.15
  381.6 1.6 fusion.7
  383.2 3.0 dynamic_update_slice.16
  386.2 1.7 fusion.5
  387.9 3.3 dynamic_update_slice.17
  391.2 1.6 fusion.3
  392.8 3.2 dynamic_update_slice.18
  396.0 1.6 fusion.1
  397.7 3.2 dynamic_update_slice.19
  400.9 2.2 slice.69
  403.1 0.0 reduce-scatter.3.cloned.1.call-update
  403.2 0.0 reduce-scatter.5.cloned.1.call-start
  403.2 33.9 %reduce-scatter.3.cloned.1.call-done = f32[64,512]{1,0:T(8,128)} async-done(((f32[512,512]{1,0:T(8,128)}), f32[64,512]{1,0:T(8,128)}) %reduce-scatter.3.cloned.1.call-update) | async-done | bytes 131088 | tf_op jit(solution)/shard_map/reduce_scatter | solution.py:49
  437.1 0.0 reduce-scatter.5.cloned.1.call-update
  437.1 21.7 %reduce-scatter.5.cloned.1.call-done = f32[16,512]{1,0:T(8,128)} async-done(((f32[64,512]{1,0:T(8,128)}), f32[16,512]{1,0:T(8,128)}) %reduce-scatter.5.cloned.1.call-update) | async-done | bytes 32784 | tf_op jit(solution)/shard_map/reduce_scatter | solution.py:50
  (1 shorter events, 0.0 us)
Async XLA Ops:
  6.5 81.6 %copy-start = (bf16[5,128,2304]{2,1,0:T(8,128)(2,1)S(1)}, bf16[5,128,2304]{2,1,0:T(8,128)(2,1)}, u32[]{:S(2)}) copy-start(bf16[5,128,2304]{2,1,0:T(8,128)(2,1)} %param.7) | copy-start | bytes 8847364
  6.5 81.6 %all-gather.2.cloned.1.call-start = ((), (), s32[]{:S(2)}) async-start(), calls=%async_computation.2 | async-start | bytes 15261696 | tf_op jit(solution)/shard_map/all_gather | solution.py:16
  7.3 429.9 %reduce-scatter.3.cloned.1.call-start = ((), (), s32[]{:S(2)}) async-start(), calls=%async_computation.3 | async-start | bytes 1179648 | tf_op jit(solution)/shard_map/reduce_scatter | solution.py:49
  403.2 55.7 %reduce-scatter.5.cloned.1.call-start = ((), (), s32[]{:S(2)}) async-start(), calls=%async_computation.4 | async-start | bytes 163840 | tf_op jit(solution)/shard_map/reduce_scatter | solution.py:50
Sparse Core Ops, SparseCore 0:
  9.2 78.8 all-gather.1
  403.3 33.7 reduce-scatter.2
  439.4 19.4 reduce-scatter.4
where the time goes:
time: 467 us; the launch traced here: 465 us
  blocking collectives  259 us (55%)
  waiting for transfers between devices  124 us (27%)
  local copies, waits for them, and re-layouts  26.4 us (6%)
  matrix products  24.3 us (5%)
  between operations  22.3 us (5%)
  other arithmetic  9.5 us (2%)
    psum x1, blocking collectives, per_device(): projected = lax.psum(masked, 'pw').astype(jnp.bfloat16)  259 us
    all_gather x1, waiting for transfers between devices, per_device(): lax.all_gather(eigvecs, 'band', axis=0, tiled=True)  67.3 us
    reduce_scatter x1, waiting for transfers between devices, per_device(): lax.psum_scatter(sigma_part, 'band', scatter_dimension=0, tiled=True)  33.9 us
    reduce_scatter x1, waiting for transfers between devices, per_device(): return lax.psum_scatter(by_band, 'pw', scatter_dimension=0, tiled=True)  21.7 us
    dynamic_update_slice x5, local copies, waits for them, and re-layouts, per_device(): lax.dynamic_update_slice(totals, previous + weights[index] * block_sigma[...  15.8 us
    dot_general x1, matrix products, per_device(): lax.dot_general(flat, lax.all_gather(eigvecs, 'band', axis=0, tiled=True)...  14.4 us
  transfers between devices with their start and end apart: 3, of which 3 were waited for; matrix products, arithmetic and copies ran while one was open for 1% of the time, Pallas kernels for 0%

commit v1 on v0

--- a/solution.py
+++ b/solution.py
@@ -13,7 +13,9 @@
     flat = density.reshape(slots * block, plane_rows)
     partial_proj = lax.dot_general(
         flat,
-        lax.all_gather(eigvecs, "band", axis=0, tiled=True),
+        jnp.concatenate(
+            lax.all_to_all(jnp.stack([eigvecs] * lax.axis_size("band")), "band", 0, 0), axis=0
+        ),
         (((1,), (1,)), ((), ())),
         preferred_element_type=jnp.float32,
     )

time: 467 us -> 548 us (1.17)
  waiting for transfers between devices: 124 us -> 200 us
  local copies, waits for them, and re-layouts: 26.4 us -> 32.9 us
  starting transfers between devices: 0.08 us -> 5.65 us
    all_to_all x0 -> x1, waiting for transfers between devices: none -> 139 us  [per_device(): lax.all_to_all(jnp.stack([eigvecs] * lax.axis_size('band')), 'band', 0, 0)]
    all_gather x1 -> x0, waiting for transfers between devices: 67.3 us -> none  [per_device(): lax.all_gather(eigvecs, 'band', axis=0, tiled=True)]
    another operation x0 -> x1, local copies, waits for them, and re-layouts: none -> 7.36 us  [per_device(): jnp.stack([eigvecs] * lax.axis_size('band'))]
    all_to_all x0 -> x1, starting transfers between devices: none -> 5.57 us  [per_device(): lax.all_to_all(jnp.stack([eigvecs] * lax.axis_size('band')), 'band', 0, 0)]
    psum x1, blocking collectives: 259 us -> 254 us  [per_device(): projected = lax.psum(masked, 'pw').astype(jnp.bfloat16)]
  transfers between devices with their start and end apart: 3 -> 3, of which waited for: 3 -> 3; matrix products, arithmetic and copies ran while one was open for 1% -> 0% of each run, Pallas kernels for 0% -> 0%
where the time goes in v1:
time: 548 us; the launch traced here: 547 us
  blocking collectives  254 us (46%)
  waiting for transfers between devices  200 us (36%)
  local copies, waits for them, and re-layouts  32.9 us (6%)
  matrix products  24.3 us (4%)
  between operations  22.9 us (4%)
  other arithmetic  7.4 us (1%)
  starting transfers between devices  5.65 us (1%)
    psum x1, blocking collectives, per_device(): projected = lax.psum(masked, 'pw').astype(jnp.bfloat16)  254 us
    all_to_all x1, waiting for transfers between devices, per_device(): lax.all_to_all(jnp.stack([eigvecs] * lax.axis_size('band')), 'band', 0, 0)  139 us
    reduce_scatter x1, waiting for transfers between devices, per_device(): lax.psum_scatter(sigma_part, 'band', scatter_dimension=0, tiled=True)  39 us
    reduce_scatter x1, waiting for transfers between devices, per_device(): return lax.psum_scatter(by_band, 'pw', scatter_dimension=0, tiled=True)  21.7 us
    dynamic_update_slice x5, local copies, waits for them, and re-layouts, per_device(): lax.dynamic_update_slice(totals, previous + weights[index] * block_sigma[...  15.8 us
    dot_general x1, matrix products, per_device(): lax.dot_general(flat, jnp.concatenate(lax.all_to_all(jnp.stack([eigvecs]...  14.3 us
  transfers between devices with their start and end apart: 3, of which 3 were waited for; matrix products, arithmetic and copies ran while one was open for 0% of the time, Pallas kernels for 0%

profile of v1, /device:TPU:0, one launch (start us, length us, event | category | flops | bytes accessed | tf_op | source)
XLA Modules:
  0.0 546.8 jit_solution(2530556187239317060)
XLA Ops:
  6.5 0.0 copy-start
  6.5 7.4 %stack.2 = bf16[8,368,2304]{2,1,0:T(8,128)(2,1)} broadcast(bf16[368,2304]{1,0:T(8,128)(2,1)} %param.8), dimensions={1,2} | broadcast | bytes 15261696 | tf_op jit(solution)/shard_map/stack | solution.py:17
  13.9 0.0 copy-start.1
  13.9 0.0 copy-start.3
  13.9 0.0 copy-start.4
  13.9 0.0 copy-start.2
  13.9 5.6 %all-to-all-start = ((bf16[8,368,2304]{2,1,0:T(8,128)(2,1)}), bf16[8,368,2304]{2,1,0:T(8,128)(2,1)}, u32[]{:S(2)}, u32[]{:S(2)}) async-start(bf16[8,368,2304]{2,1,0:T(8,128)(2,1)} %stack.2), calls=%async_computation | async-start | bytes 27131904 | tf_op jit(solution)/shard_map/all_to_all | solution.py:17
  19.5 0.0 reduce-scatter.3.cloned.1.call-start
  19.5 0.0 copy-done.1
  19.5 0.6 fusion.11
  29.5 0.0 copy-done.3
  29.5 0.0 copy-done.4
  29.6 0.2 select_reduce_fusion
  29.7 0.7 fusion.10
  30.4 0.0 copy-done.2
  30.4 0.1 convert_bitcast_fusion
  30.5 139.3 %all-to-all-done = bf16[8,368,2304]{2,1,0:T(8,128)(2,1)} async-done(((bf16[8,368,2304]{2,1,0:T(8,128)(2,1)}), bf16[8,368,2304]{2,1,0:T(8,128)(2,1)}, u32[]{:S(2)}, u32[]{:S(2)}) %all-to-all-start) | async-done | bytes 13565984 | tf_op jit(solution)/shard_map/all_to_all | solution.py:17
  169.8 0.0 copy-done
  169.8 14.3 %convolution_multiply_fusion = f32[640,2944]{1,0:T(8,128)} fusion(bf16[640,2304]{1,0:T(8,128)(2,1)S(1)} %bitcast.40, bf16[2944,2304]{1,0:T(8,128)(2,1)} %bitcast.2, f32[640]{0:T(1024)S(1)} %convert_bitcast_fusion), kind=kOutput, calls=%fused_computation | convolution fusion | flops 8684093440 | bytes 24054272 | tf_op jit(solution)/shard_map/dot_general | solution.py:14
  184.2 253.6 %all-reduce.1 = bf16[640,2944]{1,0:T(8,128)(2,1)} all-reduce(f32[640,2944]{1,0:T(8,128)} %convolution_multiply_fusion), channel_id=1, replica_groups=mesh['band'=8,'pw'=4] {'pw'}, use_global_device_ids=true, to_apply=%region_1.2 | all-reduce | flops 1884160 | bytes 11304960 | tf_op jit(solution)/shard_map/psum | solution.py:27
  437.8 2.7 constant_dynamic-slice_fusion
  440.5 8.0 %convolution_convert_fusion = bf16[640,736]{0,1:T(8,128)(2,1)} fusion(bf16[640,2944]{1,0:T(8,128)(2,1)} %all-reduce.1, bf16[736,2944]{1,0:T(8,128)(2,1)} %param.9), kind=kOutput, calls=%fused_computation.1 | convolution fusion | flops 2773954560 | bytes 9043968 | tf_op jit(solution)/shard_map/dot_general | solution.py:30
  448.5 2.3 copy.12
  450.7 1.9 fusion.12
  452.7 0.6 fusion.8
  453.3 1.3 broadcast_in_dim.10
  454.6 3.0 dynamic_update_slice.15
  457.6 1.7 fusion.7
  459.3 3.0 dynamic_update_slice.16
  462.3 1.5 fusion.5
  463.9 3.2 dynamic_update_slice.17
  467.1 1.6 fusion.3
  468.7 3.2 dynamic_update_slice.18
  472.0 1.6 fusion.1
  473.6 3.2 dynamic_update_slice.19
  476.9 2.3 slice.69
  479.1 0.0 reduce-scatter.3.cloned.1.call-update
  479.1 0.0 reduce-scatter.5.cloned.1.call-start
  479.2 39.0 %reduce-scatter.3.cloned.1.call-done = f32[64,512]{1,0:T(8,128)} async-done(((f32[512,512]{1,0:T(8,128)}), f32[64,512]{1,0:T(8,128)}) %reduce-scatter.3.cloned.1.call-update) | async-done | bytes 131088 | tf_op jit(solution)/shard_map/reduce_scatter | solution.py:51
  518.2 0.0 reduce-scatter.5.cloned.1.call-update
  518.3 21.7 %reduce-scatter.5.cloned.1.call-done = f32[16,512]{1,0:T(8,128)} async-done(((f32[64,512]{1,0:T(8,128)}), f32[16,512]{1,0:T(8,128)}) %reduce-scatter.5.cloned.1.call-update) | async-done | bytes 32784 | tf_op jit(solution)/shard_map/reduce_scatter | solution.py:52
  (2 shorter events, 0.0 us)
Async XLA Ops:
  6.5 163.3 %copy-start = (bf16[5,128,2304]{2,1,0:T(8,128)(2,1)S(1)}, bf16[5,128,2304]{2,1,0:T(8,128)(2,1)}, u32[]{:S(2)}) copy-start(bf16[5,128,2304]{2,1,0:T(8,128)(2,1)} %param.7) | copy-start | bytes 8847364
  13.9 5.6 %copy-start.1 = (s32[5]{0:T(128)S(1)}, s32[5]{0:T(128)}, u32[]{:S(2)}) copy-start(s32[5]{0:T(128)} %param.11) | copy-start | bytes 64
  13.9 15.6 %copy-start.3 = (f32[16]{0:T(128)S(1)}, f32[16]{0:T(128)}, u32[]{:S(2)}) copy-start(f32[16]{0:T(128)} %param.10) | copy-start | bytes 196
  13.9 15.6 %copy-start.4 = (s32[5]{0:T(128)S(1)}, s32[5]{0:T(128)}, u32[]{:S(2)}) copy-start(s32[5]{0:T(128)} %param.13) | copy-start | bytes 64
  13.9 16.5 %copy-start.2 = (s32[5]{0:T(128)S(1)}, s32[5]{0:T(128)}, u32[]{:S(2)}) copy-start(s32[5]{0:T(128)} %param.12) | copy-start | bytes 64
  13.9 155.9 %all-to-all-start = ((bf16[8,368,2304]{2,1,0:T(8,128)(2,1)}), bf16[8,368,2304]{2,1,0:T(8,128)(2,1)}, u32[]{:S(2)}, u32[]{:S(2)}) async-start(bf16[8,368,2304]{2,1,0:T(8,128)(2,1)} %stack.2), calls=%async_computation | async-start | bytes 27131904 | tf_op jit(solution)/shard_map/all_to_all | solution.py:17
  19.5 498.8 %reduce-scatter.3.cloned.1.call-start = ((), (), s32[]{:S(2)}) async-start(), calls=%async_computation.3 | async-start | bytes 1179648 | tf_op jit(solution)/shard_map/reduce_scatter | solution.py:51
  479.1 60.8 %reduce-scatter.5.cloned.1.call-start = ((), (), s32[]{:S(2)}) async-start(), calls=%async_computation.4 | async-start | bytes 163840 | tf_op jit(solution)/shard_map/reduce_scatter | solution.py:52
Sparse Core Ops, SparseCore 0:
  479.3 38.9 reduce-scatter.2
  520.5 19.4 reduce-scatter.4

commit v2 on v0

--- a/solution.py
+++ b/solution.py
@@ -22,7 +22,7 @@
         jnp.float32
     )
     masked = partial_proj * keep_rows.reshape(slots * block, 1)
-    projected = lax.psum(masked, "pw").astype(jnp.bfloat16)
+    projected = jnp.sum(lax.all_gather(masked, "pw"), axis=0).astype(jnp.bfloat16)
     width = screening.shape[0]
     own_cols = lax.dynamic_slice_in_dim(projected, lax.axis_index("pw") * width, width, 1)
     screened = lax.dot_general(

time: 467 us -> 727 us (1.56)
  waiting for transfers between devices: 124 us -> 630 us
  blocking collectives: 259 us -> 0 us
  other arithmetic: 9.5 us -> 22.9 us
    all_gather x0 -> x1, waiting for transfers between devices: none -> 494 us  [per_device(): lax.all_gather(masked, 'pw')]
    psum x1 -> x0, blocking collectives: 259 us -> none  [per_device(): projected = lax.psum(masked, 'pw').astype(jnp.bfloat16)]
    reduce_sum x0 -> x1, other arithmetic: none -> 14 us  [per_device(): jnp.sum(lax.all_gather(masked, 'pw'), axis=0).astype(jnp.bfloat16)]
    all_gather x1, waiting for transfers between devices: 67.3 us -> 79.3 us  [per_device(): lax.all_gather(eigvecs, 'band', axis=0, tiled=True)]
  transfers between devices with their start and end apart: 3 -> 4, of which waited for: 3 -> 4; matrix products, arithmetic and copies ran while one was open for 1% -> 0% of each run, Pallas kernels for 0% -> 0%
where the time goes in v2:
time: 727 us; the launch traced here: 725 us
  waiting for transfers between devices  630 us (87%)
  local copies, waits for them, and re-layouts  25.7 us (4%)
  matrix products  23.5 us (3%)
  other arithmetic  22.9 us (3%)
  between operations  22.9 us (3%)
    all_gather x1, waiting for transfers between devices, per_device(): lax.all_gather(masked, 'pw')  494 us
    all_gather x1, waiting for transfers between devices, per_device(): lax.all_gather(eigvecs, 'band', axis=0, tiled=True)  79.3 us
    reduce_scatter x1, waiting for transfers between devices, per_device(): lax.psum_scatter(sigma_part, 'band', scatter_dimension=0, tiled=True)  34.4 us
    reduce_scatter x1, waiting for transfers between devices, per_device(): return lax.psum_scatter(by_band, 'pw', scatter_dimension=0, tiled=True)  21.6 us
    dynamic_update_slice x5, local copies, waits for them, and re-layouts, per_device(): lax.dynamic_update_slice(totals, previous + weights[index] * block_sigma[...  15.8 us
  transfers between devices with their start and end apart: 4, of which 4 were waited for; matrix products, arithmetic and copies ran while one was open for 0% of the time, Pallas kernels for 0%

profile of v2, /device:TPU:0, one launch (start us, length us, event | category | flops | bytes accessed | tf_op | source)
XLA Modules:
  0.0 725.3 jit_solution(6339932580336313007)
XLA Ops:
  6.5 0.0 copy-start
  6.5 0.0 all-gather.4.cloned.1.call-start
  6.5 0.7 all-gather.4.cloned.1.call-update
  7.3 0.0 all-gather.6.cloned.1.call-start
  7.3 0.8 broadcast_compare_fusion
  8.1 0.7 convert_bitcast_fusion
  8.8 79.3 %all-gather.4.cloned.1.call-done = bf16[2944,2304]{1,0:T(8,128)(2,1)} async-done(((bf16[368,2304]{1,0:T(8,128)(2,1)}), bf16[2944,2304]{1,0:T(8,128)(2,1)}) %all-gather.4.cloned.1.call-update) | async-done | bytes 13565968 | tf_op jit(solution)/shard_map/all_gather | solution.py:16
  88.1 0.0 copy-done
  88.1 14.4 %convolution_multiply_fusion = f32[640,2944]{1,0:T(8,128)} fusion(bf16[640,2304]{1,0:T(8,128)(2,1)S(1)} %bitcast.40, bf16[2944,2304]{1,0:T(8,128)(2,1)} %all-gather.4.cloned.1.call-done, f32[640]{0:T(1024)S(1)} %convert_bitcast_fusion), kind=kOutput, calls=%fused_computation | convolution fusion | flops 8684093440 | bytes 24054272 | tf_op jit(solution)/shard_map/dot_general | solution.py:14
  102.5 0.0 copy-start.2
  102.5 0.0 copy-start.3
  102.5 0.0 copy-start.4
  102.5 0.0 all-gather.6.cloned.1.call-update
  102.6 0.0 reduce-scatter.3.cloned.1.call-start
  102.6 0.6 copy-done.2
  103.2 0.7 fusion.11
  113.6 0.0 copy-done.3
  113.6 0.0 copy-done.4
  113.6 0.2 select_reduce_fusion
  113.8 0.7 fusion.10
  114.5 494.1 %all-gather.6.cloned.1.call-done = f32[2560,2944]{1,0:T(8,128)} async-done(((f32[640,2944]{1,0:T(8,128)}), f32[2560,2944]{1,0:T(8,128)}) %all-gather.6.cloned.1.call-update) | async-done | bytes 30146576 | tf_op jit(solution)/shard_map/all_gather | solution.py:25
  608.5 14.0 %reduce_sum.19 = bf16[640,2944]{1,0:T(8,128)(2,1)} reduce(f32[4,640,2944]{2,1,0:T(8,128)} %bitcast.41, f32[]{:T(128)} %constant.7.clone.1), dimensions={0}, to_apply=%region_1.2 | reduce | flops 5652480 | bytes 33914884 | tf_op jit(solution)/shard_map/reduce_sum | solution.py:25
  622.6 2.7 constant_dynamic-slice_fusion
  625.2 7.0 convolution_convert_fusion
  632.2 1.7 copy.12
  634.0 0.0 copy-start.1
  634.0 2.1 fusion.12
  636.1 0.7 fusion.8
  636.7 1.3 broadcast_in_dim.10
  638.0 3.0 dynamic_update_slice.15
  641.1 1.6 fusion.7
  642.7 3.1 dynamic_update_slice.16
  645.8 1.7 fusion.5
  647.4 3.2 dynamic_update_slice.17
  650.7 1.6 fusion.3
  652.3 3.2 dynamic_update_slice.18
  655.5 1.6 fusion.1
  657.2 3.3 dynamic_update_slice.19
  660.4 2.3 slice.69
  662.7 0.0 reduce-scatter.3.cloned.1.call-update
  662.7 0.0 reduce-scatter.5.cloned.1.call-start
  662.8 34.4 %reduce-scatter.3.cloned.1.call-done = f32[64,512]{1,0:T(8,128)} async-done(((f32[512,512]{1,0:T(8,128)}), f32[64,512]{1,0:T(8,128)}) %reduce-scatter.3.cloned.1.call-update) | async-done | bytes 131088 | tf_op jit(solution)/shard_map/reduce_scatter | solution.py:49
  697.2 0.0 reduce-scatter.5.cloned.1.call-update
  697.2 21.6 %reduce-scatter.5.cloned.1.call-done = f32[16,512]{1,0:T(8,128)} async-done(((f32[64,512]{1,0:T(8,128)}), f32[16,512]{1,0:T(8,128)}) %reduce-scatter.5.cloned.1.call-update) | async-done | bytes 32784 | tf_op jit(solution)/shard_map/reduce_scatter | solution.py:50
  718.8 0.0 copy-done.1
  (1 shorter events, 0.0 us)
Async XLA Ops:
  6.5 81.6 %copy-start = (bf16[5,128,2304]{2,1,0:T(8,128)(2,1)S(1)}, bf16[5,128,2304]{2,1,0:T(8,128)(2,1)}, u32[]{:S(2)}) copy-start(bf16[5,128,2304]{2,1,0:T(8,128)(2,1)} %param.7) | copy-start | bytes 8847364
  6.5 81.6 %all-gather.4.cloned.1.call-start = ((), (), s32[]{:S(2)}) async-start(), calls=%async_computation.2 | async-start | bytes 15261696 | tf_op jit(solution)/shard_map/all_gather | solution.py:16
  7.3 601.3 %all-gather.6.cloned.1.call-start = ((), (), s32[]{:S(2)}) async-start(), calls=%async_computation.5 | async-start | bytes 37683200 | tf_op jit(solution)/shard_map/all_gather | solution.py:25
  102.5 0.7 copy-start.2
  102.5 11.1 %copy-start.3 = (s32[5]{0:T(128)S(1)}, s32[5]{0:T(128)}, u32[]{:S(2)}) copy-start(s32[5]{0:T(128)} %param.13) | copy-start | bytes 64
  102.5 11.1 %copy-start.4 = (f32[16]{0:T(128)S(1)}, f32[16]{0:T(128)}, u32[]{:S(2)}) copy-start(f32[16]{0:T(128)} %param.10) | copy-start | bytes 196
  102.6 594.6 %reduce-scatter.3.cloned.1.call-start = ((), (), s32[]{:S(2)}) async-start(), calls=%async_computation.3 | async-start | bytes 1179648 | tf_op jit(solution)/shard_map/reduce_scatter | solution.py:49
  634.0 84.8 %copy-start.1 = (bf16[5,128,2304]{2,1,0:T(8,128)(2,1)S(1)}, bf16[5,128,2304]{2,1,0:T(8,128)(2,1)}, u32[]{:S(2)}) copy-start(bf16[5,128,2304]{2,1,0:T(8,128)(2,1)} %param.7) | copy-start | bytes 8847364
  662.7 56.0 %reduce-scatter.5.cloned.1.call-start = ((), (), s32[]{:S(2)}) async-start(), calls=%async_computation.4 | async-start | bytes 163840 | tf_op jit(solution)/shard_map/reduce_scatter | solution.py:50
Sparse Core Ops, SparseCore 0:
  9.2 78.8 all-gather.3
  102.7 505.8 all-gather.5
  662.9 34.2 reduce-scatter.2
  699.3 19.4 reduce-scatter.4
